TPU v7x, 128 devices: a whole 4x4x4 slice. The times are simulated.
128 devices in a mesh: row: 8 (over y, core), col: 16 (over x, z).
Axes of the slice: x: 4, y: 4, z: 4, core: 2. Of those that a mesh axis runs over, the one named last changes fastest.
Arguments:
- density: float32 [8192, 65536], P('row', 'col'), may hold values from 0 to 1
- design_mask: int32 [64, 512], P('row', 'col'), may hold values 0 or 1
- rebalance: int32 [32768], replicated, may hold values from 0 to 32767, as said below
Outputs:
- balanced: bfloat16 [32768, 128, 128], P(('row', 'col'))
- constraint: float32 [], replicated
Inputs may be any that keep to these rules, and one draw needn't show every extreme that they name: `rebalance`: A permutation of the 32768 block numbers. Of the blocks that one device holds, the ones that land among one device's output blocks number exactly 2 or none.
All inputs are finite; a program needn't handle non-finite values. No bound on the sum of `design_mask` on one device may be relied on, other than what follows from the above.
Results may differ from a plain program's by a relative error of at most 0.001.
Values may be sent and summed in bfloat16 or wider, within the bound.
A program may use at most 192 MiB of HBM per device.

v0:
```python
import jax
import jax.numpy as jnp
from jax import lax
from jax.sharding import Mesh
from jax.sharding import PartitionSpec as P

BS = 128
RADIUS = 16
ROW = ("row_0", "row_1")
COL = ("col_0", "col_1")
ROW_COL = ("row_0", "row_1", "col_0", "col_1")


SHARPNESS = 32.0
THRESHOLD = 0.5
VOLUME_TARGET = 0.4


def with_halo(shard, sides, width):
    for axis, dim in sides:
        devices, length = (lax.axis_size(axis), shard.shape[dim])
        up = [(i, (i + 1) % devices) for i in range(devices - 1)]
        down = [(j, i) for i, j in up]
        last = lax.slice_in_dim(shard, length - width, length, axis=dim)
        initial = lax.slice_in_dim(shard, 0, width, axis=dim)
        before = lax.ppermute(last, axis, up)
        after = lax.ppermute(initial, axis, down)
        shard = jnp.concatenate([before, shard, after], axis=dim)
    return shard


def by_axis(shard, axes):
    for axis in axes:
        shard = lax.psum(shard, axis)
    return shard


def cut_along(shard, dim, devices):
    shape = shard.shape
    parts = shard.reshape(*shape[:dim], devices, shape[dim] // devices, *shape[dim + 1 :])
    return jnp.moveaxis(parts, dim, 0)


def in_order(parts, dim):
    shape = list(parts.shape[1:])
    shape[dim] *= parts.shape[0]
    return jnp.moveaxis(parts, 0, dim).reshape(shape)


def exchange_both(shard, axis, axes, splits, concats):
    sizes = [lax.axis_size(a) for a in axes]
    parts = cut_along(shard, splits[0], sizes[0])
    parts = jnp.moveaxis(cut_along(parts, splits[1] + 1, sizes[1]), 0, 1)
    inside = parts.shape[2:]
    parts = parts.reshape(-1, *inside)
    parts = lax.all_to_all(parts, axis, split_axis=0, concat_axis=0, tiled=True)
    parts = in_order(parts.reshape(*sizes, *inside), concats[0] + 1)
    return in_order(parts, concats[1])


def filter_taps():
    sigma = RADIUS / 4.0
    offsets = jnp.arange(2 * RADIUS + 1, dtype=jnp.float32) - RADIUS
    raw_taps = jnp.exp(-offsets * offsets / (2.0 * sigma * sigma))
    return raw_taps / jnp.sum(raw_taps)


def band_matrix(weights, shift):
    inner = jnp.arange(BS, dtype=jnp.int32)
    lag = inner[:, None] + shift - inner[None, :]
    taps_index = jnp.arange(2 * RADIUS + 1, dtype=jnp.int32)
    picks = (lag[:, :, None] == taps_index[None, None, :]).astype(jnp.float32)
    return jnp.sum(picks * weights[None, None, :], axis=2)


def filter_first(extended, band_near, band_next):
    height, width = extended.shape
    block_count = (height - 2 * RADIUS) // BS
    padded = jnp.pad(extended, ((0, BS - 2 * RADIUS), (0, 0)))
    blocks = padded.reshape(block_count + 1, BS, width)
    result = jnp.einsum(
        "ij,bic->bjc", band_near, blocks[:block_count], precision=lax.Precision.HIGHEST
    )
    result = result + jnp.einsum(
        "ij,bic->bjc", band_next, blocks[1:], precision=lax.Precision.HIGHEST
    )
    return result.reshape(block_count * BS, width)


def filter_last(extended, band_near, band_next):
    height, width = extended.shape
    block_count = (width - 2 * RADIUS) // BS
    padded = jnp.pad(extended, ((0, 0), (0, BS - 2 * RADIUS)))
    blocks = padded.reshape(height, block_count + 1, BS)
    result = jnp.einsum(
        "mbi,ij->mbj", blocks[:, :block_count], band_near, precision=lax.Precision.HIGHEST
    )
    result = result + jnp.einsum(
        "mbi,ij->mbj", blocks[:, 1:], band_next, precision=lax.Precision.HIGHEST
    )
    return result.reshape(height, block_count * BS)


def per_device(density, design_mask, rebalance):
    tile_rows, tile_cols = density.shape
    weights = filter_taps()
    band_near = band_matrix(weights, 0)
    band_next = band_matrix(weights, BS)
    extended = with_halo(density, ((ROW, 0),), RADIUS)
    along_rows = filter_first(extended, band_near, band_next)
    widened = with_halo(along_rows, ((COL, 1),), RADIUS)
    filtered = filter_last(widened, band_near, band_next)
    mask_rows, mask_cols = design_mask.shape
    cell_mask = jnp.broadcast_to(
        design_mask.astype(jnp.float32)[:, None, :, None], (mask_rows, BS, mask_cols, BS)
    )
    cell_mask = cell_mask.reshape(tile_rows, tile_cols)
    lower = jnp.tanh(SHARPNESS * THRESHOLD)
    upper = jnp.tanh(SHARPNESS * (1.0 - THRESHOLD))
    projected = cell_mask * (lower + jnp.tanh(SHARPNESS * (filtered - THRESHOLD))) / (lower + upper)
    total_volume = by_axis(jnp.sum(projected), ROW_COL)
    row_count = lax.axis_size(ROW)
    col_count = lax.axis_size(COL)
    grid_cells = float(tile_rows * tile_cols * row_count * col_count)
    constraint = total_volume / grid_cells / VOLUME_TARGET - 1.0
    block_count = mask_rows * mask_cols
    device_count = row_count * col_count
    capacity = max(2, block_count // device_count)
    tiles = projected.astype(jnp.bfloat16).reshape(mask_rows, BS, mask_cols, BS)
    tiles = tiles.transpose(0, 2, 1, 3).reshape(block_count, BS * BS)
    local_index = jnp.arange(block_count, dtype=jnp.int32)
    block_row = lax.axis_index(ROW) * mask_rows + local_index // mask_cols
    block_col = lax.axis_index(COL) * mask_cols + local_index % mask_cols
    global_id = block_row * (mask_cols * col_count) + block_col
    everywhere = jnp.arange(rebalance.shape[0], dtype=jnp.int32)
    matches = rebalance[None, :] == global_id[:, None]
    position = jnp.sum(jnp.where(matches, everywhere[None, :], 0), axis=1)
    target_dev = position // block_count
    target_slot = position % block_count
    earlier = (target_dev[:, None] == target_dev[None, :]) & (
        local_index[None, :] < local_index[:, None]
    )
    send_rank = jnp.sum(earlier.astype(jnp.int32), axis=1)
    send_row = target_dev * capacity + send_rank
    buffer_index = jnp.arange(device_count * capacity, dtype=jnp.int32)
    chosen = buffer_index[:, None] == send_row[None, :]
    outgoing = jnp.dot(
        chosen.astype(jnp.bfloat16), tiles, preferred_element_type=jnp.float32
    ).astype(jnp.bfloat16)
    out_slots = jnp.sum(jnp.where(chosen, target_slot[None, :] + 1, 0), axis=1) - 1
    grid_send = outgoing.reshape(row_count, col_count, capacity, BS * BS)
    grid_slots = out_slots.reshape(row_count, col_count, capacity)
    arrived, arrived_slots = (
        exchange_both(grid_send, ROW_COL, (ROW, COL), (0, 1), (0, 1)),
        exchange_both(grid_slots, ROW_COL, (ROW, COL), (0, 1), (0, 1)),
    )
    arrived = arrived.reshape(device_count * capacity, BS * BS)
    arrived_slots = arrived_slots.reshape(device_count * capacity)
    placing = (arrived_slots[None, :] == local_index[:, None]).astype(jnp.bfloat16)
    balanced = jnp.dot(placing, arrived, preferred_element_type=jnp.float32).astype(jnp.bfloat16)
    return (balanced.reshape(block_count, BS, BS), constraint)


def solution(mesh):
    finer = Mesh(mesh.devices.reshape(4, 2, 4, 4), ("row_0", "row_1", "col_0", "col_1"))
    in_specs = (P(ROW, COL), P(ROW, COL), P())
    out_specs = (P(ROW_COL, None, None), P())
    return jax.shard_map(
        per_device, mesh=finer, in_specs=in_specs, out_specs=out_specs, check_vma=False
    )
```

profile of v0, /device:TPU:0, one launch (start us, length us, event | category | flops | bytes accessed | tf_op | source)
XLA Modules:
  0.0 421.0 jit_solution(1817748898629907539)
XLA Ops:
  1.7 1.3 collective-permute-start
  3.0 1.3 collective-permute-start.1
  5.1 5.5 %select_reduce_fusion = s32[256]{0:T(256)S(1)} fusion(s32[32768]{0:T(1024)} %param.5, s32[256]{0:T(256)S(1)} %fusion.19), kind=kLoop, calls=%fused_computation | loop fusion | flops 25165568 | bytes 133120 | tf_op jit(solution)/shard_map/reduce_sum | solution.py:137
  12.1 21.1 %pad_maximum_fusion = (f32[1024,4096]{1,0:T(8,128)}, f32[1024,4096]{1,0:T(8,128)}) fusion(f32[1024,4096]{1,0:T(8,128)} %param.3, f32[16,4096]{1,0:T(8,128)S(1)} %collective-permute-done, f32[16,4096]{1,0:T(8,128)S(1)} %collective-permute-done.1), kind=kLoop, calls=%fused_computation.12 | loop fusion | flops 33554432 | bytes 50855936 | tf_op jit(solution)/shard_map/concatenate | solution.py:28
  33.2 32.0 %fusion.12 = f32[8,4096,128]{1,2,0:T(8,128)} fusion(f32[8,128,4096]{2,1,0:T(8,128)} %bitcast.65, f32[128,128]{1,0:T(8,128)S(1)} %get-tuple-element.3), kind=kOutput, calls=%fused_computation.37 | convolution fusion | flops 6442450944 | bytes 33619968 | tf_op jit(solution)/shard_map/ij,bic->bjc/dot_general | solution.py:84
  65.2 23.8 %convolution_add_fusion = f32[8,4096,128]{1,2,0:T(8,128)} fusion(f32[8,4096,128]{1,2,0:T(8,128)} %fusion.12, f32[8,128,4096]{2,1,0:T(8,128)} %bitcast.67, f32[128,128]{1,0:T(8,128)S(1)} %get-tuple-element.2), kind=kOutput, calls=%fused_computation.18 | convolution fusion | flops 6446645248 | bytes 50397184 | tf_op jit(solution)/shard_map/ij,bic->bjc/dot_general | solution.py:81
  89.0 17.5 %copy.32 = f32[1024,4096]{0,1:T(8,128)} copy(f32[1024,4096]{1,0:T(8,128)} %bitcast.68) | data formatting | bytes 33554432 | tf_op jit(solution)/shard_map/reshape | solution.py:87
  107.3 4.4 %collective-permute-start.2 = (f32[1024,16]{0,1:T(8,128)S(1)}, f32[1024,16]{0,1:T(8,128)S(1)}, u32[]{:S(2)}, u32[]{:S(2)}) collective-permute-start(f32[1024,16]{0,1:T(8,128)S(1)} %get-tuple-element.6), channel_id=1, source_target_pairs={{0,1},{1,2},{2,3},{3,4},{4,5},{5,6},{6,7},{7,8},{8,9},{9,10},{10,1... | collective-permute-start | bytes 196616 | tf_op jit(solution)/shard_map/ppermute | solution.py:26
  111.7 1.3 collective-permute-start.3
  113.8 14.5 %all-to-all-start = ((s32[128,1,1,2]{3,2,1,0:T(1,128)}), s32[128,1,1,2]{3,2,1,0:T(1,128)S(1)}, u32[]{:S(2)}, u32[]{:S(2)}) async-start(s32[128,1,1,2]{3,2,1,0:T(1,128)} %bitcast), calls=%async_computation | async-start | bytes 131072 | tf_op jit(solution)/shard_map/all_to_all | solution.py:56
  128.6 7.0 %select_maximum_fusion = f32[1024,4224]{0,1:T(8,128)S(1)} fusion(f32[1024,16]{0,1:T(8,128)S(1)} %collective-permute-done.3, f32[1024,4096]{0,1:T(8,128)} %copy.32, f32[1024,16]{0,1:T(8,128)S(1)} %collective-permute-done.2), kind=kLoop, calls=%fused_computation.3 | loop fusion | flops 25952256 | bytes 34209792 | tf_op jit(solution)/shard_map/concatenate | solution.py:28
  135.6 29.6 %fusion.10 = f32[1024,32,128]{2,0,1:T(8,128)} fusion(f32[1024,33,128]{0,2,1:T(8,128)S(1)} %bitcast.63, f32[128,128]{1,0:T(8,128)S(1)} %get-tuple-element.3), kind=kOutput, calls=%fused_computation.35 | convolution fusion | flops 6442450944 | bytes 34144256 | tf_op jit(solution)/shard_map/mbi,ij->mbj/dot_general | solution.py:98
  165.2 39.0 %multiply_reduce_fusion = (f32[]{:T(128)}, f32[1024,32,128]{2,0,1:T(8,128)}) fusion(f32[1024,32]{0,1:T(8,128)S(1)} %bitcast.72, f32[1024,32,128]{2,0,1:T(8,128)} %fusion.10, f32[1024,33,128]{0,2,1:T(8,128)S(1)} %bitcast.64, f32[128,128]{1,0:T(8,128)S(1)} %get-tuple-element.2), kind=kOutput, calls=%fused_computation.16 | convolution fusion | flops 6471811072 | bytes 51052548 | tf_op jit(solution)/shard_map/mbi,ij->mbj/dot_general | solution.py:95
  204.3 6.9 %fusion.3 = bf16[8,128,32,128]{3,1,2,0:T(8,128)(2,1)S(1)} fusion(f32[8,128,32,128]{3,1,0,2:T(8,128)} %bitcast.66, f32[8,32]{1,0:T(8,128)S(1)} %convert_element_type.25), kind=kLoop, calls=%fused_computation.15 | loop fusion | flops 12582912 | bytes 25166848 | tf_op jit(solution)/shard_map/convert_element_type | solution.py:129
  211.2 21.0 %convolution_convert_fusion.1 = bf16[256,16384]{1,0:T(8,128)(2,1)} fusion(bf16[32,8,128,128]{3,2,1,0:T(8,128)(2,1)S(1)} %bitcast.70, s32[256]{0:T(256)S(1)} %multiply_add_fusion), kind=kOutput, calls=%fused_computation.2 | convolution fusion | flops 2151743488 | bytes 16778240 | tf_op jit(solution)/shard_map/dot_general | solution.py:147
  232.1 14.1 %reshape_transpose_transpose_reshape_reshape_reshape.4 = bf16[128,1,1,2,16384]{4,3,0,2,1:T(2,128)(2,1)} reshape(bf16[256,16384]{1,0:T(8,128)(2,1)} %convolution_convert_fusion.1) | data formatting | bytes 16777216 | tf_op jit(solution)/shard_map/reshape;transpose;transpose;reshape;reshape;reshape | solution.py:55
  246.2 10.4 %all-to-all-start.1 = ((bf16[128,1,1,2,16384]{4,3,2,1,0:T(2,128)(2,1)}), bf16[128,1,1,2,16384]{4,3,2,1,0:T(2,128)(2,1)}, u32[]{:S(2)}, u32[]{:S(2)}) async-start(bf16[128,1,1,2,16384]{4,3,2,1,0:T(2,128)(2,1)} %bitcast.69), calls=%async_computation.1 | async-start | bytes 16777216 | tf_op jit(solution)/shard_map/all_to_all | solution.py:56
  256.6 100.1 %psum.28 = f32[]{:T(128)} all-reduce(f32[]{:T(128)} %get-tuple-element.12), channel_id=1, replica_groups=mesh['row_0'=4,'row_1'=2,'col_0'=4,'col_1'=4] {'row_0'}, use_global_device_ids=true, to_apply=%region_7.8 | all-reduce | flops 1 | bytes 8 | tf_op jit(solution)/shard_map/psum | solution.py:34
  356.8 3.1 psum.29
  359.8 13.6 %psum.30 = f32[]{:T(128)} all-reduce(f32[]{:T(128)} %psum.29), channel_id=1, replica_groups=mesh['row_0'=4,'row_1'=2,'col_0'=4,'col_1'=4] {'col_0'}, use_global_device_ids=true, to_apply=%region_9.10 | all-reduce | flops 1 | bytes 8 | tf_op jit(solution)/shard_map/psum | solution.py:34
  373.6 14.0 %psum.31 = f32[]{:T(128)} all-reduce(f32[]{:T(128)} %psum.30), channel_id=1, replica_groups=mesh['row_0'=4,'row_1'=2,'col_0'=4,'col_1'=4] {'col_1'}, use_global_device_ids=true, to_apply=%region_10.11 | all-reduce | flops 1 | bytes 8 | tf_op jit(solution)/shard_map/psum | solution.py:34
  388.3 13.1 %reshape_reshape.3 = bf16[256,16384]{1,0:T(8,128)(2,1)} reshape(bf16[8,16,1,2,16384]{4,3,1,0,2:T(2,128)(2,1)} %bitcast.21) | data formatting | bytes 16777216 | tf_op jit(solution)/shard_map/reshape;reshape | solution.py:157
  401.4 8.9 %fusion.6 = bf16[32,8,128,128]{3,1,2,0:T(8,128)(2,1)} fusion(bf16[256,16384]{1,0:T(8,128)(2,1)} %reshape_reshape.3, s32[256]{0:T(256)S(1)} %eq.95), kind=kOutput, calls=%fused_computation.21 | convolution fusion | flops 2151743488 | bytes 16778240 | tf_op jit(solution)/shard_map/dot_general | solution.py:160
  410.3 9.4 %copy.47 = bf16[32,8,128,128]{3,2,1,0:T(8,128)(2,1)} copy(bf16[32,8,128,128]{3,1,2,0:T(8,128)(2,1)} %fusion.6) | data formatting | bytes 16777216
  (27 shorter events, 5.2 us)
Async XLA Ops:
  1.7 10.4 %collective-permute-start = (f32[16,4096]{1,0:T(8,128)S(1)}, f32[16,4096]{1,0:T(8,128)S(1)}, u32[]{:S(2)}, u32[]{:S(2)}) collective-permute-start(f32[16,4096]{1,0:T(8,128)S(1)} %get-tuple-element.8), channel_id=1, source_target_pairs={{0,16},{16,32},{32,48},{48,64},{64,80},{80,96},{96,112},{1,17},{17... | collective-permute-start | bytes 786440 | tf_op jit(solution)/shard_map/ppermute | solution.py:26
  3.0 9.1 %collective-permute-start.1 = (f32[16,4096]{1,0:T(8,128)S(1)}, f32[16,4096]{1,0:T(8,128)S(1)}, u32[]{:S(2)}, u32[]{:S(2)}) collective-permute-start(f32[16,4096]{1,0:T(8,128)S(1)} %get-tuple-element.9), channel_id=1, source_target_pairs={{16,0},{32,16},{48,32},{64,48},{80,64},{96,80},{112,96},{17,1},{33... | collective-permute-start | bytes 786440 | tf_op jit(solution)/shard_map/ppermute | solution.py:27
  89.0 39.3 %copy-start = (s32[8,32]{1,0:T(8,128)S(1)}, s32[8,32]{1,0:T(8,128)}, u32[]{:S(2)}) copy-start(s32[8,32]{1,0:T(8,128)} %param.4) | copy-start | bytes 3076
  107.3 21.2 %collective-permute-start.2 = (f32[1024,16]{0,1:T(8,128)S(1)}, f32[1024,16]{0,1:T(8,128)S(1)}, u32[]{:S(2)}, u32[]{:S(2)}) collective-permute-start(f32[1024,16]{0,1:T(8,128)S(1)} %get-tuple-element.6), channel_id=1, source_target_pairs={{0,1},{1,2},{2,3},{3,4},{4,5},{5,6},{6,7},{7,8},{8,9},{9,10},{10,1... | collective-permute-start | bytes 196616 | tf_op jit(solution)/shard_map/ppermute | solution.py:26
  111.7 16.8 %collective-permute-start.3 = (f32[1024,16]{0,1:T(8,128)S(1)}, f32[1024,16]{0,1:T(8,128)S(1)}, u32[]{:S(2)}, u32[]{:S(2)}) collective-permute-start(f32[1024,16]{0,1:T(8,128)S(1)} %get-tuple-element.7), channel_id=1, source_target_pairs={{1,0},{2,1},{3,2},{4,3},{5,4},{6,5},{7,6},{8,7},{9,8},{10,9},{11,1... | collective-permute-start | bytes 196616 | tf_op jit(solution)/shard_map/ppermute | solution.py:27
  113.8 132.4 %all-to-all-start = ((s32[128,1,1,2]{3,2,1,0:T(1,128)}), s32[128,1,1,2]{3,2,1,0:T(1,128)S(1)}, u32[]{:S(2)}, u32[]{:S(2)}) async-start(s32[128,1,1,2]{3,2,1,0:T(1,128)} %bitcast), calls=%async_computation | async-start | bytes 131072 | tf_op jit(solution)/shard_map/all_to_all | solution.py:56
  246.2 142.1 %all-to-all-start.1 = ((bf16[128,1,1,2,16384]{4,3,2,1,0:T(2,128)(2,1)}), bf16[128,1,1,2,16384]{4,3,2,1,0:T(2,128)(2,1)}, u32[]{:S(2)}, u32[]{:S(2)}) async-start(bf16[128,1,1,2,16384]{4,3,2,1,0:T(2,128)(2,1)} %bitcast.69), calls=%async_computation.1 | async-start | bytes 16777216 | tf_op jit(solution)/shard_map/all_to_all | solution.py:56
where the time goes:
time: 427 us; the launch traced here: 421 us
  matrix products  154 us (36%)
  blocking collectives  131 us (31%)
  local copies, waits for them, and re-layouts  57 us (13%)
  other arithmetic  42.8 us (10%)
  starting transfers between devices  33.2 us (8%)
    psum x4, blocking collectives, by_axis(): shard = lax.psum(shard, axis)  131 us
    dot_general x1, matrix products, filter_last(): jnp.einsum('mbi,ij->mbj', blocks[:, :block_count], band_near, precision=l...  39 us
    dot_general x1, matrix products, filter_first(): jnp.einsum('ij,bic->bjc', band_next, blocks[1:], precision=lax.Precision....  32 us
    dot_general x1, matrix products, filter_last(): jnp.einsum('mbi,ij->mbj', blocks[:, 1:], band_next, precision=lax.Precisi...  29.6 us
    concatenate x2, other arithmetic, with_halo(): shard = jnp.concatenate([before, shard, after], axis=dim)  28.2 us
    all_to_all x2, starting transfers between devices, exchange_both(): parts = lax.all_to_all(parts, axis, split_axis=0, concat_axis=0, tiled=True)  24.9 us
    dot_general x1, matrix products, filter_first(): jnp.einsum('ij,bic->bjc', band_near, blocks[:block_count], precision=lax....  23.8 us
    dot_general x1, matrix products, per_device(): jnp.dot(chosen.astype(jnp.bfloat16), tiles, preferred_element_type=jnp.fl...  21 us
  transfers between devices with their start and end apart: 6, of which 0 were waited for; matrix products, arithmetic and copies ran while one was open for 30% of the time, Pallas kernels for 0%

commit v1 on v0

v1 whole, which is shorter than its diff:
```python
import functools

import jax
import jax.numpy as jnp
import numpy as np
from jax import lax
from jax.experimental import pallas as pl
from jax.experimental.pallas import tpu as pltpu
from jax.sharding import PartitionSpec as P

BS = 128
RADIUS = 16
SHARPNESS = 32.0
THRESHOLD = 0.5
VOLUME_TARGET = 0.4
MESH = pl.DeviceIdType.MESH

KR = 8
KC = 32
SIDE = 4
GROUPS = 4
WIN = BS + 2 * RADIUS
ROWS = KR * BS
COLS = KC * BS
UNROLL = 8

ROUTES = ((0, 1, 2), (1, 2, 0), (2, 0, 1))
PARTS = ((0, 48), (48, 48), (96, 32))
CHUNKS = tuple(
    (g, g % 2, ROUTES[i], *PARTS[(i + g) % 3]) for g in range(GROUPS) for i in range(3)
)
NCH = len(CHUNKS)


def filter_taps():
    sigma = RADIUS / 4.0
    offsets = np.arange(2 * RADIUS + 1, dtype=np.float64) - RADIUS
    raw = np.exp(-offsets * offsets / (2.0 * sigma * sigma))
    return raw / raw.sum()


def taps_at(lag):
    taps = filter_taps()
    inside = (lag >= 0) & (lag <= 2 * RADIUS)
    return np.where(inside, taps[np.clip(lag, 0, 2 * RADIUS)], 0.0).astype(np.float32)


def high_low(array):
    high = array.astype(jnp.bfloat16)
    low = (array - high.astype(np.float32)).astype(jnp.bfloat16)
    return high, low


def row_weights():
    lag = np.arange(WIN)[None, :] - np.arange(BS)[:, None]
    return np.concatenate(high_low(taps_at(lag)), axis=0)


def col_weights():
    lane = np.arange(BS)
    edge = np.where(lane < BS // 2, lane + BS, lane - BS)
    position = np.concatenate([lane, edge])
    lag = position[:, None] - lane[None, :] + RADIUS
    once = np.concatenate(high_low(taps_at(lag)), axis=1)
    return np.concatenate([once, once], axis=0)


def split_f32(value):
    high = value.astype(jnp.bfloat16)
    low = (value - high.astype(jnp.float32)).astype(jnp.bfloat16)
    return high, low


def fused_kernel(
    density, table, mask, w_row, w_col,
    arrived, total,
    win_top, win_bot, win, a_hi, a_lo, send, mid1, mid2, edge_out, edge_in, sums,
    load_sem, halo_send, halo_recv, edge_send, edge_recv, sum_send, sum_recv,
    out_send, out_recv, local_sem,
):
    row = lax.axis_index("row")
    col = lax.axis_index("col")
    y, core = row // 2, row % 2
    x, z = col // SIDE, col % SIDE
    me = (x, y, z)

    def device(c, k):
        return (c[1] * 2 + k, c[0] * SIDE + c[2])

    def along(axis, step):
        c = list(me)
        c[axis] = lax.rem(me[axis] + step, SIDE)
        return c

    def load(i, slot):
        return pltpu.make_async_copy(
            density.at[pl.ds(i * BS - RADIUS, WIN)], win.at[slot], load_sem.at[slot]
        )

    top_load = pltpu.make_async_copy(
        density.at[pl.ds(0, BS + RADIUS)], win_top.at[pl.ds(RADIUS, BS + RADIUS)], load_sem.at[2]
    )
    bot_load = pltpu.make_async_copy(
        density.at[pl.ds(ROWS - BS - RADIUS, BS + RADIUS)],
        win_bot.at[pl.ds(0, BS + RADIUS)],
        load_sem.at[3],
    )
    load(1, 0).start()
    load(2, 1).start()
    top_load.start()
    bot_load.start()

    row_next, row_prev = lax.rem(row + 1, 8), lax.rem(row + 7, 8)
    col_next, col_prev = lax.rem(col + 1, 16), lax.rem(col + 15, 16)
    barrier = pltpu.get_barrier_semaphore()
    count = 0
    for axis in range(3):
        for step in range(1, SIDE):
            for k in range(2):
                pl.semaphore_signal(
                    barrier, inc=1, device_id=device(along(axis, step), lax.rem(core + k, 2)),
                    device_id_type=MESH,
                )
                count += 1
    for target in (device(me, 1 - core), (row, col_next), (row, col_prev)):
        pl.semaphore_signal(barrier, inc=1, device_id=target, device_id_type=MESH)
        count += 1
    pl.semaphore_wait(barrier, count)

    down = pltpu.make_async_remote_copy(
        src_ref=density.at[pl.ds(ROWS - RADIUS, RADIUS)], dst_ref=win_top.at[pl.ds(0, RADIUS)],
        send_sem=halo_send.at[0], recv_sem=halo_recv.at[0],
        device_id=(row_next, col), device_id_type=MESH,
    )
    up = pltpu.make_async_remote_copy(
        src_ref=density.at[pl.ds(0, RADIUS)], dst_ref=win_bot.at[pl.ds(BS + RADIUS, RADIUS)],
        send_sem=halo_send.at[1], recv_sem=halo_recv.at[1],
        device_id=(row_prev, col), device_id_type=MESH,
    )
    down.start()
    up.start()

    taps_row = w_row[...]

    def first(window, i, tile):
        value = window[:, pl.ds(pl.multiple_of(tile * BS, BS), BS)]
        high, low = split_f32(value)
        got = jnp.dot(
            taps_row, jnp.concatenate([high, low], axis=1), preferred_element_type=jnp.float32
        )
        part = got[:BS] + got[BS:]
        value = part[:, :BS] + part[:, BS:]
        high, low = split_f32(value)
        a_hi[i, tile + 1] = high
        a_lo[i, tile + 1] = low
        return value

    def edges(i, left, right):
        lane = lax.broadcasted_iota(jnp.int32, (BS, BS), 1) // RADIUS == i
        for side, (tile, first_lane) in enumerate(((left, 0), (right, BS - RADIUS))):
            moved = pltpu.roll(tile, (RADIUS * i - first_lane) % BS, 1)
            edge_out[side] = jnp.where(lane, moved, edge_out[side])

    edge_out[...] = jnp.zeros_like(edge_out)

    def tiles(window, i, begin, end):
        def body(step, carry):
            for u in range(UNROLL):
                first(window, i, begin + step * UNROLL + u)
            return carry

        lax.fori_loop(0, (end - begin) // UNROLL, body, 0)

    def whole_row(window, i):
        tiles(window, i, 0, KC)

    def edge_tile(i, tile):
        return a_hi[i, tile + 1].astype(jnp.float32) + a_lo[i, tile + 1].astype(jnp.float32)

    for i in range(1, KR - 1):
        slot = (i - 1) % 2
        load(i, slot).wait()
        whole_row(win.at[slot], i)
        edges(i, edge_tile(i, 0), edge_tile(i, KC - 1))
        if i + 2 < KR - 1:
            load(i + 2, slot).start()

    top_load.wait()
    down.wait_recv()
    keep = jnp.where(row > 0, 1.0, 0.0).astype(jnp.float32)
    win_top[pl.ds(0, RADIUS), :] = win_top[pl.ds(0, RADIUS), :] * keep
    whole_row(win_top, 0)
    edges(0, edge_tile(0, 0), edge_tile(0, KC - 1))
    bot_load.wait()
    up.wait_recv()
    keep = jnp.where(row < 7, 1.0, 0.0).astype(jnp.float32)
    win_bot[pl.ds(BS + RADIUS, RADIUS), :] = win_bot[pl.ds(BS + RADIUS, RADIUS), :] * keep
    whole_row(win_bot, KR - 1)
    edges(KR - 1, edge_tile(KR - 1, 0), edge_tile(KR - 1, KC - 1))

    to_left = pltpu.make_async_remote_copy(
        src_ref=edge_out.at[0], dst_ref=edge_in.at[1],
        send_sem=edge_send.at[0], recv_sem=edge_recv.at[1],
        device_id=(row, col_prev), device_id_type=MESH,
    )
    to_right = pltpu.make_async_remote_copy(
        src_ref=edge_out.at[1], dst_ref=edge_in.at[0],
        send_sem=edge_send.at[1], recv_sem=edge_recv.at[0],
        device_id=(row, col_next), device_id_type=MESH,
    )
    to_left.start()
    to_right.start()
    to_right.wait_recv()
    to_left.wait_recv()
    for side, (inside, tile, first_lane) in enumerate(
        ((col > 0, 0, BS - RADIUS), (col < 15, KC + 1, 0))
    ):
        value = edge_in[side] * jnp.where(inside, 1.0, 0.0).astype(jnp.float32)
        high, low = split_f32(value)
        high, low = high.astype(jnp.float32), low.astype(jnp.float32)
        for i in range(KR):
            shift = (first_lane - RADIUS * i) % BS
            a_hi[i, tile] = pltpu.roll(high, shift, 1).astype(jnp.bfloat16)
            a_lo[i, tile] = pltpu.roll(low, shift, 1).astype(jnp.bfloat16)

    right_half = lax.broadcasted_iota(jnp.int32, (BS, BS), 1) < BS // 2
    lower = float(np.tanh(np.float32(SHARPNESS * THRESHOLD)))
    upper = float(np.tanh(np.float32(SHARPNESS * (1.0 - THRESHOLD))))

    def second(block):
        i = block // KC
        tile = lax.rem(block, KC)
        pieces = []
        for ref in (a_hi, a_lo):
            pieces.append(ref[i, tile + 1])
            pieces.append(jnp.where(right_half, ref[i, tile + 2], ref[i, tile]))
        got = jnp.dot(
            jnp.concatenate(pieces, axis=1), w_col[...], preferred_element_type=jnp.float32
        )
        filtered = got[:, :BS] + got[:, BS:]
        scale = mask[block].astype(jnp.float32) * (1.0 / (lower + upper))
        return scale * (lower + jnp.tanh(SHARPNESS * (filtered - THRESHOLD)))

    def view(ref, g, picks, begin, rows):
        index = [picks.get(d, slice(None)) for d in range(3)]
        return ref.at[(g, *index, pl.ds(begin, rows), slice(None))]

    def remote(src, dst, axis, step, flip, sem):
        pltpu.make_async_remote_copy(
            src_ref=src, dst_ref=dst, send_sem=out_send.at[sem], recv_sem=out_recv.at[sem],
            device_id=device(along(axis, step), lax.rem(core + flip, 2)), device_id_type=MESH,
        ).start()

    def wait(sem, ref):
        pltpu.make_async_copy(ref, ref, sem).wait()

    others = pl.ds(1, SIDE - 1)
    steps = (1, 3, 2)

    def hop1(j):
        g, flip, (a, b, c), begin, rows = CHUNKS[j]
        for step in ((0,) if flip else ()) + steps:
            remote(
                view(send, g, {a: step}, begin, rows), view(mid1, g, {a: step}, begin, rows),
                a, step, flip, j,
            )

    def got1(j):
        g, flip, (a, b, c), begin, rows = CHUNKS[j]
        return view(mid1, g, {} if flip else {a: others}, begin, rows)

    def hop2(j):
        g, flip, (a, b, c), begin, rows = CHUNKS[j]
        wait(out_recv.at[j], got1(j))
        for step in steps:
            if flip:
                pairs = ((mid1, {b: step}),)
            else:
                pairs = ((mid1, {b: step, a: others}), (send, {b: step, a: 0}))
            for ref, picks in pairs:
                remote(
                    view(ref, g, picks, begin, rows), view(mid2, g, picks, begin, rows),
                    b, step, 0, NCH + j,
                )

    def got2(j):
        g, flip, (a, b, c), begin, rows = CHUNKS[j]
        return view(mid2, g, {b: others}, begin, rows)

    def hop3(j):
        g, flip, (a, b, c), begin, rows = CHUNKS[j]
        wait(out_recv.at[NCH + j], got2(j))
        for step in steps + (0,):
            pairs = [(mid2, {c: step, b: others})]
            if flip:
                pairs.append((mid1, {c: step, b: 0}))
            else:
                pairs.append((mid1, {c: step, b: 0, a: others}))
                pairs.append((send, {c: step, b: 0, a: 0}))
            for ref, picks in pairs:
                src, dst = view(ref, g, picks, begin, rows), view(arrived, g, picks, begin, rows)
                if step:
                    remote(src, dst, c, step, 0, 2 * NCH + j)
                else:
                    pltpu.make_async_copy(src, dst, local_sem.at[0]).start()

    def got3(j):
        g, flip, (a, b, c), begin, rows = CHUNKS[j]
        return view(arrived, g, {c: others}, begin, rows)

    volume = jnp.zeros((8, BS), jnp.float32)
    for g in range(GROUPS):

        def body(step, acc, g=g):
            dx = step // 2
            for u in range(UNROLL):
                dy, dz = lax.rem(step, 2) * 2 + u // SIDE, u % SIDE
                target_row = lax.rem(y + dy, SIDE) * 2 + lax.rem(core + g, 2)
                target_col = lax.rem(x + dx, SIDE) * SIDE + (z + dz) % SIDE
                target = target_row * 16 + target_col
                block = table[target * 2 + g // 2]
                value = second(block)
                send[g, dx, dy, dz] = value.astype(jnp.bfloat16)
                acc = acc + jnp.sum(value.reshape(BS // 8, 8, BS), axis=0)
            return acc

        volume = lax.fori_loop(0, 64 // UNROLL, body, volume)
        for j in range(3 * g, 3 * g + 3):
            hop1(j)

    def spread(stage, own, slots, targets):
        first_slot = (0, 8, 12)[stage]
        sums[first_slot + own] = volume_parts[stage]
        for target in targets:
            pltpu.make_async_remote_copy(
                src_ref=sums.at[first_slot + own], dst_ref=sums.at[first_slot + own],
                send_sem=sum_send.at[stage], recv_sem=sum_recv.at[stage],
                device_id=target, device_id_type=MESH,
            ).start()

    def collect(stage, slots):
        first_slot = (0, 8, 12)[stage]
        for sem in (sum_recv, sum_send):
            wait(sem.at[stage], sums.at[pl.ds(first_slot, slots - 1)])
        out = sums[first_slot]
        for s in range(1, slots):
            out = out + sums[first_slot + s]
        return out

    volume_parts = [volume]
    spread(
        0, x * 2 + core, 8,
        [device(along(0, s), lax.rem(core + k, 2)) for s in range(SIDE) for k in range(2) if s or k],
    )
    for j in range(NCH):
        hop2(j)
    volume_parts.append(collect(0, 8))
    spread(1, y, 4, [device(along(1, s), core) for s in range(1, SIDE)])
    for j in range(NCH):
        hop3(j)
    volume_parts.append(collect(1, 4))
    spread(2, z, 4, [device(along(2, s), core) for s in range(1, SIDE)])
    all_volume = jnp.sum(collect(2, 4))
    cells = float(ROWS * COLS * 128)
    constraint = all_volume / cells / VOLUME_TARGET - 1.0
    total[...] = jnp.full((8, BS), constraint, jnp.float32)

    for j in range(NCH):
        wait(out_recv.at[2 * NCH + j], got3(j))
    for j in range(NCH):
        wait(out_send.at[j], got1(j))
        wait(out_send.at[NCH + j], got2(j))
        wait(out_send.at[2 * NCH + j], got3(j))
        g, flip, (a, b, c), begin, rows = CHUNKS[j]
        wait(local_sem.at[0], view(arrived, g, {c: 0}, begin, rows))
    for copy in (down, up, to_left, to_right):
        copy.wait_send()


def place_kernel(index, arrived, out, held, in_sem, out_sem):
    parts = 8
    per = KR * KC // parts

    def start(j, carry):
        pltpu.make_async_copy(arrived.at[index[j]], held.at[j], in_sem.at[j // per]).start()
        return carry

    lax.fori_loop(0, KR * KC, start, 0, unroll=8)
    for p in range(parts):
        piece = pl.ds(p * per, per)
        pltpu.make_async_copy(arrived.at[piece], held.at[piece], in_sem.at[p]).wait()
        pltpu.make_async_copy(held.at[piece], out.at[piece], out_sem.at[p]).start()
    for p in range(parts):
        piece = pl.ds(p * per, per)
        pltpu.make_async_copy(held.at[piece], out.at[piece], out_sem.at[p]).wait()


def tables(rebalance):
    row, col = lax.axis_index("row"), lax.axis_index("col")
    ids = rebalance.reshape(128, KR * KC)

    def owner(ids):
        block_row, block_col = ids // (KC * 16), ids % (KC * 16)
        device = block_row // KR * 16 + block_col // KC
        return device, block_row % KR * KC + block_col % KC

    device, local = owner(ids)
    me = row * 16 + col
    mine = device == me
    low = jnp.min(jnp.where(mine, local, 1 << 20), axis=1)
    high = jnp.max(jnp.where(mine, local, -1), axis=1)
    table = jnp.stack([low, high], axis=1).reshape(-1)

    own = lax.dynamic_slice_in_dim(ids, me, 1, 0)[0]
    source, block = owner(own)
    earlier = (source[:, None] == source[None, :]) & (block[None, :] < block[:, None])
    rank = jnp.sum(earlier.astype(jnp.int32), axis=1)
    source_row, source_col = source // 16, source % 16
    dy = (row // 2 - source_row // 2) % SIDE
    flip = (row + source_row) % 2
    dx = (col // SIDE - source_col // SIDE) % SIDE
    dz = (col - source_col) % SIDE
    index = (rank * 2 + flip) * 64 + dx * 16 + dy * SIDE + dz
    return table, index


def per_device(density, design_mask, rebalance):
    table, index = tables(rebalance)
    smem = pl.BlockSpec(memory_space=pltpu.SMEM)
    vmem = pl.BlockSpec(memory_space=pltpu.VMEM)
    anywhere = pl.BlockSpec(memory_space=pl.ANY)
    exchange = (GROUPS, SIDE, SIDE, SIDE, BS, BS)
    window = pltpu.VMEM((WIN, COLS), jnp.float32)
    field = pltpu.VMEM((KR, KC + 2, BS, BS), jnp.bfloat16)
    dma = pltpu.SemaphoreType.DMA
    arrived, total = pl.pallas_call(
        fused_kernel,
        out_shape=(
            jax.ShapeDtypeStruct(exchange, jnp.bfloat16),
            jax.ShapeDtypeStruct((8, BS), jnp.float32),
        ),
        in_specs=[anywhere, smem, smem, vmem, vmem],
        out_specs=(anywhere, vmem),
        scratch_shapes=[
            window, window, pltpu.VMEM((2, WIN, COLS), jnp.float32), field, field,
            *[pltpu.VMEM(exchange, jnp.bfloat16)] * 3,
            pltpu.VMEM((2, BS, BS), jnp.float32), pltpu.VMEM((2, BS, BS), jnp.float32),
            pltpu.VMEM((16, 8, BS), jnp.float32),
            dma((4,)), dma((2,)), dma((2,)), dma((2,)), dma((2,)), dma((3,)), dma((3,)),
            dma((3 * NCH,)), dma((3 * NCH,)), dma((1,)),
        ],
        compiler_params=pltpu.CompilerParams(
            collective_id=0, has_side_effects=True, vmem_limit_bytes=63 * 2**20
        ),
        name="filter_exchange",
    )(
        density, table, design_mask.reshape(-1),
        jnp.asarray(row_weights()), jnp.asarray(col_weights()),
    )
    balanced = pl.pallas_call(
        place_kernel,
        out_shape=jax.ShapeDtypeStruct((KR * KC, BS, BS), jnp.bfloat16),
        in_specs=[smem, anywhere],
        out_specs=anywhere,
        scratch_shapes=[pltpu.VMEM((KR * KC, BS, BS), jnp.bfloat16), dma((8,)), dma((8,))],
        compiler_params=pltpu.CompilerParams(vmem_limit_bytes=16 * 2**20),
        name="place_blocks",
    )(index, arrived.reshape(KR * KC, BS, BS))
    return balanced, total[0, 0]


def solution(mesh):
    return jax.shard_map(
        per_device, mesh=mesh,
        in_specs=(P("row", "col"), P("row", "col"), P()),
        out_specs=(P(("row", "col"), None, None), P()),
        check_vma=False,
    )
```

time: 427 us -> 151 us (0.35); the launches traced: 421 us -> 151 us
  matrix products: 154 us -> 0 us
  Pallas kernels: 0 us -> 142 us
  blocking collectives: 131 us -> 0 us
  local copies, waits for them, and re-layouts: 57 us -> 7.62 us
  other arithmetic: 42.8 us -> 0.79 us
  starting transfers between devices: 33.2 us -> 0 us
    dot_general x6 -> x0, matrix products: 154 us -> none  [the longest x1 39 us: filter_last(): jnp.einsum('mbi,ij->mbj', blocks[:, :block_count], band_near, precision=l...]
    pallas_call x0 -> x2, Pallas kernels: none -> 142 us  [the longest x1 125 us: per_device(): pl.pallas_call(fused_kernel, out_shape=(jax.ShapeDtypeStruct(exchange, jn...]
    psum x4 -> x0, blocking collectives: 131 us -> none  [by_axis(): shard = lax.psum(shard, axis)]
    concatenate x2 -> x0, other arithmetic: 28.2 us -> none  [with_halo(): shard = jnp.concatenate([before, shard, after], axis=dim)]
    another operation x2 -> x1, local copies, waits for them, and re-layouts: 27.1 us -> 0.11 us  [tables(): table = jnp.stack([low, high], axis=1).reshape(-1)]
    all_to_all x2 -> x0, starting transfers between devices: 24.9 us -> none  [exchange_both(): parts = lax.all_to_all(parts, axis, split_axis=0, concat_axis=0, tiled=True)]
    reshape x1 -> x3, local copies, waits for them, and re-layouts: 17.5 us -> 2.94 us  [the longest x1 1.29 us: per_device(): design_mask.reshape(-1)]
    ppermute x4 -> x0, starting transfers between devices: 8.28 us -> none  [the longest x2 5.69 us: with_halo(): before = lax.ppermute(last, axis, up)]
  transfers between devices with their start and end apart: 6 -> 0, of which waited for: 0 -> 0; matrix products, arithmetic and copies ran while one was open for 30% -> 0% of each run, Pallas kernels for 0% -> 0%
where the time goes in v1:
time: 151 us
  Pallas kernels  142 us (94%)
  local copies, waits for them, and re-layouts  7.62 us (5%)
    pallas_call x1, Pallas kernels, per_device(): pl.pallas_call(fused_kernel, out_shape=(jax.ShapeDtypeStruct(exchange, jn...  125 us
    pallas_call x1, Pallas kernels, per_device(): pl.pallas_call(place_kernel, out_shape=jax.ShapeDtypeStruct((KR * KC, BS,...  16.5 us
    unnamed x2, local copies, waits for them, and re-layouts  3.38 us

profile of v1, /device:TPU:0, one launch (start us, length us, event | category | flops | bytes accessed | tf_op | source)
XLA Modules:
  0.0 151.0 jit_solution(10462861758269521780)
XLA Ops:
  0.7 1.3 reshape.137.mask
  1.9 0.9 reshape.135
  2.9 0.5 select_reduce_fusion.1
  3.5 0.2 convert_reduce_fusion
  3.7 0.1 copy.8
  3.8 0.7 reshape.136.table
  4.6 125.4 %filter_exchange.1 = (bf16[4,4,4,4,128,128]{5,4,3,2,1,0:T(8,128)(2,1)}, f32[8,128]{1,0:T(8,128)}) custom-call(f32[1024,4096]{1,0:T(8,128)} %density.1, s32[256]{0:T(256)} %reshape.136.table, s32[256]{0:T(256)} %reshape.137.mask, bf16[256,160]{1,0:T(8,128)(2,1)} %constant.229.clone.w_row, bf16[512,256]{1,0:T(8,128)(2,1)} %constant.230.clone.w_col), custom_call_target="tpu_custom_call" | custom-call | tf_op jit(solution)/shard_map/filter_exchange/pallas_call | solution.py:436
  129.9 1.2 slice.3
  131.1 0.0 copy-start
  131.1 3.4 %copy-done = bf16[4,4,4,4,128,128]{5,4,3,2,1,0:T(8,128)(2,1)S(1)} copy-done((bf16[4,4,4,4,128,128]{5,4,3,2,1,0:T(8,128)(2,1)S(1)}, bf16[4,4,4,4,128,128]{5,4,3,2,1,0:T(8,128)(2,1)}, u32[]{:S(2)}) %copy-start) | copy-done | bytes 8388632
  134.5 16.5 %place_blocks.1 = bf16[256,128,128]{2,1,0:T(8,128)(2,1)} custom-call(s32[256]{0:T(256)S(1)} %fusion.13.index, bf16[256,128,128]{2,1,0:T(8,128)(2,1)S(1)} %bitcast.7), custom_call_target="tpu_custom_call" | custom-call | tf_op jit(solution)/shard_map/place_blocks/pallas_call | solution.py:460
  (7 shorter events, 0.1 us)
Async XLA Ops:
  131.1 3.4 %copy-start = (bf16[4,4,4,4,128,128]{5,4,3,2,1,0:T(8,128)(2,1)S(1)}, bf16[4,4,4,4,128,128]{5,4,3,2,1,0:T(8,128)(2,1)}, u32[]{:S(2)}) copy-start(bf16[4,4,4,4,128,128]{5,4,3,2,1,0:T(8,128)(2,1)} %get-tuple-element.4) | copy-start | bytes 25165828

commit v2 on v1

v2 whole, which is shorter than its diff:
```python
import functools

import jax
import jax.numpy as jnp
import numpy as np
from jax import lax
from jax.experimental import pallas as pl
from jax.experimental.pallas import tpu as pltpu
from jax.sharding import PartitionSpec as P

BS = 128
RADIUS = 16
SHARPNESS = 32.0
THRESHOLD = 0.5
VOLUME_TARGET = 0.4
MESH = pl.DeviceIdType.MESH

KR = 8
KC = 32
SIDE = 4
GROUPS = 4
WIN = BS + 2 * RADIUS
ROWS = KR * BS
COLS = KC * BS
GROUPS_IN = ROWS // RADIUS
BATCH = 16
PACK = 4
STEPS = (1, 3, 2, 0)
OTHERS = pl.ds(0, SIDE - 1)
HOME = SIDE - 1

ROUTES = ((0, 1, 2), (1, 2, 0), (2, 0, 1))
PARTS = ((0, 48), (48, 48), (96, 32))
CHUNKS = tuple(
    (g, g % 2, ROUTES[i], *PARTS[(i + g) % 3]) for g in range(GROUPS) for i in range(3)
)
NCH = len(CHUNKS)


def filter_taps():
    sigma = RADIUS / 4.0
    offsets = np.arange(2 * RADIUS + 1, dtype=np.float64) - RADIUS
    raw = np.exp(-offsets * offsets / (2.0 * sigma * sigma))
    return raw / raw.sum()


def taps_at(lag):
    taps = filter_taps()
    inside = (lag >= 0) & (lag <= 2 * RADIUS)
    return np.where(inside, taps[np.clip(lag, 0, 2 * RADIUS)], 0.0).astype(np.float32)


def high_low(array):
    high = array.astype(jnp.bfloat16)
    low = (array - high.astype(np.float32)).astype(jnp.bfloat16)
    return high, low


def row_weights():
    lag = np.arange(WIN)[None, :] - np.arange(BS)[:, None]
    once = np.concatenate(high_low(taps_at(lag)), axis=0)
    return np.concatenate([once, once], axis=1)


def col_weights():
    lane = np.arange(BS)
    edge = np.where(lane < BS // 2, lane + BS, lane - BS)
    position = np.concatenate([lane, edge])
    lag = position[:, None] - lane[None, :] + RADIUS
    once = np.concatenate(high_low(taps_at(lag)), axis=1)
    return np.concatenate([once, once], axis=0)


def split_f32(value):
    high = value.astype(jnp.bfloat16)
    low = (value - high.astype(jnp.float32)).astype(jnp.bfloat16)
    return high, low


def fused_kernel(
    density, rebalance, w_row_in, w_col_in, mask,
    arrived, slots, total,
    field, rim, along_rows, ids, w_row, w_col, keys, table, send, mid1, mid2, edge_out, edge_in, sums,
    load_sem, aux_sem, table_sem, halo_send, halo_recv, sum_send, sum_recv,
    out_send, out_recv, local_sem,
):
    row = lax.axis_index("row")
    col = lax.axis_index("col")
    y, core = row // 2, row % 2
    x, z = col // SIDE, col % SIDE
    me = (x, y, z)
    my_id = row * 16 + col

    def device(c, k):
        return (c[1] * 2 + k, c[0] * SIDE + c[2])

    def along(axis, step):
        c = list(me)
        c[axis] = lax.rem(me[axis] + step, SIDE)
        return c

    inner = pl.ds(1, GROUPS_IN)
    aux = [
        pltpu.make_async_copy(src, dst, aux_sem.at[n])
        for n, (src, dst) in enumerate(((rebalance, ids), (w_row_in, w_row), (w_col_in, w_col)))
    ]
    loads = [
        pltpu.make_async_copy(
            density.at[:, :, pl.ds(tile * BS, BS)], field.at[tile + 1, inner], load_sem.at[n]
        )
        for n, tile in enumerate((0, KC - 1, *range(1, KC - 1)))
    ]
    edge_loads, loads = loads[:2], loads[2:]
    for copy in (*edge_loads, *aux, *loads):
        copy.start()

    next_row, prev_row = lax.rem(row + 1, 8), lax.rem(row + 7, 8)
    next_col, prev_col = lax.rem(col + 1, 16), lax.rem(col + 15, 16)
    greeted = [
        device(along(axis, step), lax.rem(core + k, 2))
        for axis in range(3) for step in range(1, SIDE) for k in range(2)
    ]
    greeted += [device(me, 1 - core), (row, next_col), (row, prev_col)]
    greeted += [(r, c) for r in (next_row, prev_row) for c in (next_col, prev_col)]
    barrier = pltpu.get_barrier_semaphore()
    for target in greeted:
        pl.semaphore_signal(barrier, inc=1, device_id=target, device_id_type=MESH)

    for copy in edge_loads:
        copy.wait()
    lane_group = lax.broadcasted_iota(jnp.int32, (BS, BS), 1) // RADIUS
    for side, (tile, first_lane) in enumerate(((0, 0), (KC - 1, BS - RADIUS))):
        packed = jnp.zeros((BS, BS), jnp.float32)
        for i in range(KR):
            value = field[tile + 1, pl.ds(1 + i * 8, 8)].reshape(BS, BS)
            moved = pltpu.roll(value, (RADIUS * i - first_lane) % BS, 1)
            packed = jnp.where(lane_group == i, moved, packed)
        edge_out[side] = packed

    pl.semaphore_wait(barrier, len(greeted))

    last = GROUPS_IN - 1
    own_left, own_right = pl.ds(0, BS), pl.ds(COLS - BS, BS)
    wide, left, right = pl.ds(BS, COLS), pl.ds(0, BS), pl.ds(BS + COLS, BS)
    halo = [
        (edge_out.at[0], edge_in.at[1], (row, prev_col)),
        (edge_out.at[1], edge_in.at[0], (row, next_col)),
        (density.at[last], rim.at[0, :, wide], (next_row, col)),
        (density.at[0], rim.at[1, :, wide], (prev_row, col)),
        (density.at[last, :, own_right], rim.at[0, :, left], (next_row, next_col)),
        (density.at[last, :, own_left], rim.at[0, :, right], (next_row, prev_col)),
        (density.at[0, :, own_right], rim.at[1, :, left], (prev_row, next_col)),
        (density.at[0, :, own_left], rim.at[1, :, right], (prev_row, prev_col)),
    ]
    halo = [
        pltpu.make_async_remote_copy(
            src_ref=src, dst_ref=dst, send_sem=halo_send.at[n], recv_sem=halo_recv.at[n],
            device_id=target, device_id_type=MESH,
        )
        for n, (src, dst, target) in enumerate(halo)
    ]
    for copy in halo:
        copy.start()

    for copy in aux:
        copy.wait()

    def owner(number):
        return (number >> 12) * 16 + ((number >> 5) & 15)

    def local(number):
        return ((number >> 9) & 7) * KC + (number & (KC - 1))

    none = 1 << 20
    turned = ids[...].T
    mine = owner(turned) == my_id
    block = local(turned)
    keys[pl.ds(0, 1), :] = jnp.min(jnp.where(mine, block, none), 0, keepdims=True)
    keys[pl.ds(1, 1), :] = jnp.max(jnp.where(mine, block, -1), 0, keepdims=True)
    to_table = pltpu.make_async_copy(keys, table, table_sem.at[0])
    to_table.start()
    low, high = jnp.full((1, BS), none, jnp.int32), jnp.full((1, BS), -1, jnp.int32)
    source = lax.broadcasted_iota(jnp.int32, (BS, BS), 1)
    for half in range(2):
        own = jnp.broadcast_to(ids[pl.ds(my_id * 2 + half, 1), :], (BS, BS)).T
        slot = lax.broadcasted_iota(jnp.int32, (BS, BS), 0) + half * BS
        key = local(own) * 256 + slot
        here = owner(own) == source
        low = jnp.minimum(low, jnp.min(jnp.where(here, key, none), 0, keepdims=True))
        high = jnp.maximum(high, jnp.max(jnp.where(here, key, -1), 0, keepdims=True))
    slots[...] = jnp.zeros_like(slots)
    slots[pl.ds(0, 1), :] = low & 255
    slots[pl.ds(1, 1), :] = high & 255

    for copy in halo:
        copy.wait_recv()
    for copy in loads:
        copy.wait()

    def kept(condition):
        return jnp.where(condition, 1.0, 0.0).astype(jnp.float32)

    keep_side = (kept(col > 0), kept(col < 15))
    for side, (tile, first_lane) in enumerate(((0, BS - RADIUS), (KC + 1, 0))):
        value = edge_in[side] * keep_side[side]
        for i in range(KR):
            moved = pltpu.roll(value, (first_lane - RADIUS * i) % BS, 1)
            field[tile, pl.ds(1 + i * 8, 8)] = moved.reshape(8, RADIUS, BS)
    for end, (group, keep) in enumerate(((0, kept(row > 0)), (GROUPS_IN + 1, kept(row < 7)))):
        for tile in range(KC + 2):
            scale = keep * keep_side[tile > 0] if tile in (0, KC + 1) else keep
            field[tile, group] = rim[end, :, tile * BS : (tile + 1) * BS] * scale
    to_table.wait()

    right_half = lax.broadcasted_iota(jnp.int32, (WIN, BS), 1) < BS // 2
    quarter = lax.broadcasted_iota(jnp.int32, (WIN, BS), 1) // (2 * RADIUS)
    lower = float(np.tanh(np.float32(SHARPNESS * THRESHOLD)))
    upper = float(np.tanh(np.float32(SHARPNESS * (1.0 - THRESHOLD))))

    def turn(n):
        return 2 * RADIUS * n + RADIUS

    def first_filter(tiles, uses):
        window = jnp.concatenate(tiles, axis=1)
        got = jnp.dot(
            w_row[...], jnp.concatenate(split_f32(window), axis=0),
            preferred_element_type=jnp.float32,
        )
        got = got[:BS] + got[BS:]
        for n, tile_uses in enumerate(uses):
            for u, offset, shift in tile_uses:
                value = got[:, n * BS : (n + 1) * BS]
                if shift:
                    value = pltpu.roll(value, shift, 1)
                for m, piece in enumerate(split_f32(value)):
                    at = 2 * BS * m + offset
                    along_rows[u * BS : (u + 1) * BS, at : at + BS] = piece

    def batch(blocks):
        waiting = []
        packed = None
        for u, block in enumerate(blocks):
            tile = block & (KC - 1)
            group = (block >> 5) * 8

            def part(offset):
                return jnp.concatenate(
                    [field[tile + offset, group + n] for n in range(WIN // RADIUS)], axis=0
                )

            waiting.append((part(1), [(u, 0, 0)]))
            n = u % PACK
            edge = pltpu.roll(jnp.where(right_half, part(2), part(0)), turn(n), 1)
            packed = jnp.where(quarter == n, edge, packed) if n else edge
            if n == PACK - 1:
                uses = [(u - n + m, BS, (BS - turn(m)) % BS) for m in range(PACK)]
                waiting.append((packed, uses))
            while len(waiting) > 1:
                first_filter(*zip(waiting.pop(0), waiting.pop(0)))
        got = jnp.dot(along_rows[...], w_col[...], preferred_element_type=jnp.float32)
        filtered = got[:, :BS] + got[:, BS:]
        value = lower + jnp.tanh(SHARPNESS * (filtered - THRESHOLD))
        out = []
        for u, block in enumerate(blocks):
            scale = mask[block >> 5, block & (KC - 1)].astype(jnp.float32) * (1.0 / (lower + upper))
            out.append(scale * value[u * BS : (u + 1) * BS])
        return out

    def source_block(rank, target):
        pair = (table[rank, target * 2], table[rank, target * 2 + 1])
        return (jnp.minimum(*pair) if rank == 0 else jnp.maximum(*pair)) & (KR * KC - 1)

    def fill(g, half_x, half_y, acc):
        def step(half, n):
            return 3 - 3 * half if n else 1 + half

        places, blocks = [], []
        for u in range(BATCH):
            n, m, p = u // 8, u // SIDE % 2, u % SIDE
            to_x, to_y = (x + step(half_x, n)) & 3, (y + step(half_y, m)) & 3
            to_z = (z + STEPS[p]) & 3
            target = (to_y * 2 + ((core + g) & 1)) * 16 + to_x * SIDE + to_z
            blocks.append(source_block(g // 2, target))
            places.append((g, 2 * half_x + n, 2 * half_y + m, p))
        for place, value in zip(places, batch(blocks)):
            send[place] = value.astype(jnp.bfloat16)
            acc = acc + jnp.sum(value.reshape(BS // 8, 8, BS), axis=0)
        return acc

    def view(ref, g, picks, begin, rows):
        index = [picks.get(d, slice(None)) for d in range(3)]
        return ref.at[(g, *index, pl.ds(begin, rows), slice(None))]

    def remote(src, dst, axis, step, flip, sem):
        pltpu.make_async_remote_copy(
            src_ref=src, dst_ref=dst, send_sem=out_send.at[sem], recv_sem=out_recv.at[sem],
            device_id=device(along(axis, step), lax.rem(core + flip, 2)), device_id_type=MESH,
        ).start()

    def wait(sem, ref):
        pltpu.make_async_copy(ref, ref, sem).wait()

    def hop1(j, half_x=None, half_y=None):
        g, flip, (a, b, c), begin, rows = CHUNKS[j]
        for p in range(SIDE if flip else HOME):
            picks = {}
            for axis, half in ((0, half_x), (1, half_y)):
                if half is not None:
                    picks[axis] = pl.ds(2 * half, 2)
                    if axis == a and p // 2 != half:
                        break
            else:
                picks[a] = p
                remote(
                    view(send, g, picks, begin, rows), view(mid1, g, picks, begin, rows),
                    a, STEPS[p], flip, j,
                )

    def got1(j):
        g, flip, (a, b, c), begin, rows = CHUNKS[j]
        return view(mid1, g, {} if flip else {a: OTHERS}, begin, rows)

    def hop2(j):
        g, flip, (a, b, c), begin, rows = CHUNKS[j]
        wait(out_recv.at[j], got1(j))
        for p in range(HOME):
            if flip:
                pairs = ((mid1, {b: p}),)
            else:
                pairs = ((mid1, {b: p, a: OTHERS}), (send, {b: p, a: HOME}))
            for ref, picks in pairs:
                remote(
                    view(ref, g, picks, begin, rows), view(mid2, g, picks, begin, rows),
                    b, STEPS[p], 0, NCH + j,
                )

    def got2(j):
        g, flip, (a, b, c), begin, rows = CHUNKS[j]
        return view(mid2, g, {b: OTHERS}, begin, rows)

    def hop3(j):
        g, flip, (a, b, c), begin, rows = CHUNKS[j]
        wait(out_recv.at[NCH + j], got2(j))
        for p in range(SIDE):
            pairs = [(mid2, {c: p, b: OTHERS})]
            if flip:
                pairs.append((mid1, {c: p, b: HOME}))
            else:
                pairs.append((mid1, {c: p, b: HOME, a: OTHERS}))
                pairs.append((send, {c: p, b: HOME, a: HOME}))
            for ref, picks in pairs:
                src, dst = view(ref, g, picks, begin, rows), view(arrived, g, picks, begin, rows)
                if p != HOME:
                    remote(src, dst, c, STEPS[p], 0, 2 * NCH + j)
                else:
                    pltpu.make_async_copy(src, dst, local_sem.at[0]).start()

    def got3(j):
        g, flip, (a, b, c), begin, rows = CHUNKS[j]
        return view(arrived, g, {c: OTHERS}, begin, rows)

    def of(g):
        return range(3 * g, 3 * g + 3)

    volume = jnp.zeros((8, BS), jnp.float32)
    for g in range(GROUPS):
        if g < 2:
            for half_x in range(2):
                for half_y in range(2):
                    volume = fill(g, half_x, half_y, volume)
                    for j in of(g):
                        hop1(j, half_x, half_y)
                if g == 1 and half_x == 0:
                    for j in of(0):
                        hop2(j)
        else:
            volume = lax.fori_loop(
                0, SIDE, lambda n, acc, g=g: fill(g, n // 2, lax.rem(n, 2), acc), volume
            )
            for j in of(g):
                hop1(j)
            for j in of(g - 1):
                hop2(j)

    def spread(stage, own, slots, targets):
        first_slot = (0, 8, 12)[stage]
        sums[first_slot + own] = volume_parts[stage]
        for target in targets:
            pltpu.make_async_remote_copy(
                src_ref=sums.at[first_slot + own], dst_ref=sums.at[first_slot + own],
                send_sem=sum_send.at[stage], recv_sem=sum_recv.at[stage],
                device_id=target, device_id_type=MESH,
            ).start()

    def collect(stage, slots):
        first_slot = (0, 8, 12)[stage]
        for sem in (sum_recv, sum_send):
            wait(sem.at[stage], sums.at[pl.ds(first_slot, slots - 1)])
        out = sums[first_slot]
        for s in range(1, slots):
            out = out + sums[first_slot + s]
        return out

    volume_parts = [volume]
    spread(
        0, x * 2 + core, 8,
        [device(along(0, s), lax.rem(core + k, 2)) for s in range(SIDE) for k in range(2) if s or k],
    )
    for j in range(NCH - 3, NCH):
        hop2(j)
    volume_parts.append(collect(0, 8))
    spread(1, y, 4, [device(along(1, s), core) for s in range(1, SIDE)])
    for j in range(NCH):
        hop3(j)
    volume_parts.append(collect(1, 4))
    spread(2, z, 4, [device(along(2, s), core) for s in range(1, SIDE)])
    all_volume = jnp.sum(collect(2, 4))
    cells = float(ROWS * COLS * 128)
    constraint = all_volume / cells / VOLUME_TARGET - 1.0
    total[...] = jnp.full((8, BS), constraint, jnp.float32)

    for j in range(NCH):
        wait(out_recv.at[2 * NCH + j], got3(j))
    for j in range(NCH):
        wait(out_send.at[j], got1(j))
        wait(out_send.at[NCH + j], got2(j))
        wait(out_send.at[2 * NCH + j], got3(j))
        g, flip, (a, b, c), begin, rows = CHUNKS[j]
        wait(local_sem.at[0], view(arrived, g, {c: HOME}, begin, rows))
    for copy in halo:
        copy.wait_send()


def place_kernel(slots, total, arrived, out, constraint, sem):
    row = lax.axis_index("row")
    col = lax.axis_index("col")
    y, core, x, z = row // 2, row % 2, col // SIDE, col % SIDE

    from_x = [((x - step) & 3) * SIDE for step in STEPS]
    from_y = [((y - step) & 3) * 32 for step in STEPS]
    from_z = [(z - step) & 3 for step in STEPS]
    from_core = [((core + flip) & 1) * 16 for flip in range(2)]
    for g in range(GROUPS):
        for n in range(SIDE):
            for m in range(SIDE):
                base = from_core[g % 2] + from_x[n] + from_y[m]
                for p in range(SIDE):
                    pltpu.make_async_copy(
                        arrived.at[g, n, m, p], out.at[slots[g // 2, base + from_z[p]]], sem.at[0]
                    ).start()
    constraint[0, 0] = total[0, 0]
    pltpu.make_async_copy(out, out, sem.at[0]).wait()


def per_device(density, design_mask, rebalance):
    smem = pl.BlockSpec(memory_space=pltpu.SMEM)
    vmem = pl.BlockSpec(memory_space=pltpu.VMEM)
    anywhere = pl.BlockSpec(memory_space=pl.ANY)
    exchange = (GROUPS, SIDE, SIDE, SIDE, BS, BS)
    w_row, w_col = row_weights(), col_weights()
    dma = pltpu.SemaphoreType.DMA
    arrived, slots, total = pl.pallas_call(
        fused_kernel,
        out_shape=(
            pltpu.VMEM(exchange, jnp.bfloat16),
            pltpu.VMEM((8, BS), jnp.int32),
            pltpu.VMEM((8, BS), jnp.float32),
        ),
        in_specs=[anywhere, anywhere, anywhere, anywhere, smem],
        out_specs=(vmem, vmem, vmem),
        scratch_shapes=[
            pltpu.VMEM((KC + 2, GROUPS_IN + 2, RADIUS, BS), jnp.float32),
            pltpu.VMEM((2, RADIUS, COLS + 2 * BS), jnp.float32),
            pltpu.VMEM((BATCH * BS, 4 * BS), jnp.bfloat16),
            pltpu.VMEM((2 * BS, BS), jnp.int32),
            pltpu.VMEM(w_row.shape, jnp.bfloat16), pltpu.VMEM(w_col.shape, jnp.bfloat16),
            pltpu.VMEM((2, 2 * BS), jnp.int32), pltpu.SMEM((2, 2 * BS), jnp.int32),
            *[pltpu.VMEM(exchange, jnp.bfloat16)] * 3,
            pltpu.VMEM((2, BS, BS), jnp.float32), pltpu.VMEM((2, BS, BS), jnp.float32),
            pltpu.VMEM((16, 8, BS), jnp.float32),
            dma((KC,)), dma((3,)), dma((1,)), dma((8,)), dma((8,)), dma((3,)), dma((3,)),
            dma((3 * NCH,)), dma((3 * NCH,)), dma((1,)),
        ],
        compiler_params=pltpu.CompilerParams(
            collective_id=0, has_side_effects=True, vmem_limit_bytes=54 * 2**20
        ),
        name="filter_exchange",
    )(
        density.reshape(GROUPS_IN, RADIUS, COLS), rebalance.reshape(2 * BS, BS), jnp.asarray(w_row), jnp.asarray(w_col),
        design_mask,
    )
    balanced, constraint = pl.pallas_call(
        place_kernel,
        out_shape=(
            jax.ShapeDtypeStruct((KR * KC, BS, BS), jnp.bfloat16),
            jax.ShapeDtypeStruct((1, 1), jnp.float32),
        ),
        in_specs=[smem, smem, vmem],
        out_specs=(anywhere, smem),
        scratch_shapes=[dma((1,))],
        compiler_params=pltpu.CompilerParams(vmem_limit_bytes=10 * 2**20),
        name="place_blocks",
    )(slots, total, arrived)
    return balanced, constraint.reshape(())


def solution(mesh):
    return jax.shard_map(
        per_device, mesh=mesh,
        in_specs=(P("row", "col"), P("row", "col"), P()),
        out_specs=(P(("row", "col"), None, None), P()),
        check_vma=False,
    )
```

time: 151 us -> 119 us (0.79)
  Pallas kernels: 142 us -> 118 us
  local copies, waits for them, and re-layouts: 7.62 us -> 0 us
    pallas_call x2, Pallas kernels: 142 us -> 118 us  [the longest x1 114 us: per_device(): pl.pallas_call(fused_kernel, out_shape=(pltpu.VMEM(exchange, jnp.bfloat16...]
    unnamed x2 -> x0, local copies, waits for them, and re-layouts: 3.38 us -> none
    reshape x3 -> x0, local copies, waits for them, and re-layouts: 2.94 us -> none  [the longest x1 1.29 us: per_device(): design_mask.reshape(-1)]
where the time goes in v2:
time: 119 us
  Pallas kernels  118 us (99%)
    pallas_call x1, Pallas kernels, per_device(): pl.pallas_call(fused_kernel, out_shape=(pltpu.VMEM(exchange, jnp.bfloat16...  114 us
    pallas_call x1, Pallas kernels, per_device(): pl.pallas_call(place_kernel, out_shape=(jax.ShapeDtypeStruct((KR * KC, BS...  4.39 us

profile of v2, /device:TPU:0, one launch (start us, length us, event | category | flops | bytes accessed | tf_op | source)
XLA Modules:
  0.0 119.2 jit_solution(4662961704326856050)
XLA Ops:
  0.6 114.0 %filter_exchange.1 = (bf16[4,4,4,4,128,128]{5,4,3,2,1,0:T(8,128)(2,1)S(1)}, s32[8,128]{1,0:T(8,128)S(1)}, f32[8,128]{1,0:T(8,128)S(1)}) custom-call(f32[64,16,4096]{2,1,0:T(8,128)} %bitcast.3, s32[256,128]{1,0:T(8,128)} %bitcast.4, bf16[256,320]{1,0:T(8,128)(2,1)} %constant.4.clone.w_row_in, bf16[512,256]{1,0:T(8,128)(2,1)} %constant.5.clone.w_col_in, ...), custom_call_target="tpu_custom_call" | custom-call | tf_op jit(solution)/shard_map/filter_exchange/pallas_call | solution.py:462
  114.6 4.4 %place_blocks.1 = (bf16[256,128,128]{2,1,0:T(8,128)(2,1)}, f32[1,1]{1,0:T(1,128)}) custom-call(s32[8,128]{1,0:T(8,128)S(1)} %get-tuple-element.7.slots, f32[8,128]{1,0:T(8,128)S(1)} %get-tuple-element.8.total, bf16[4,4,4,4,128,128]{5,4,3,2,1,0:T(8,128)(2,1)S(1)} %get-tuple-element.9.arrived), custom_call_target="tpu_custom_call" | custom-call | tf_op jit(solution)/shard_map/place_blocks/pallas_call | solution.py:492

commit v3 on v2

--- a/solution.py
+++ b/solution.py
@@ -106,7 +106,7 @@
     ]
     loads = [
         pltpu.make_async_copy(
-            density.at[:, :, pl.ds(tile * BS, BS)], field.at[tile + 1, inner], load_sem.at[n]
+            density.at[:, :, pl.ds(tile * BS, BS)], field.at[tile + 1, inner], load_sem.at[min(n, 2)]
         )
         for n, tile in enumerate((0, KC - 1, *range(1, KC - 1)))
     ]
@@ -194,8 +194,8 @@
 
     for copy in halo:
         copy.wait_recv()
-    for copy in loads:
-        copy.wait()
+    bulk = field.at[pl.ds(2, KC - 2), inner]
+    pltpu.make_async_copy(bulk, bulk, load_sem.at[2]).wait()
 
     def kept(condition):
         return jnp.where(condition, 1.0, 0.0).astype(jnp.float32)
@@ -293,7 +293,7 @@
 
     def remote(src, dst, axis, step, flip, sem):
         pltpu.make_async_remote_copy(
-            src_ref=src, dst_ref=dst, send_sem=out_send.at[sem], recv_sem=out_recv.at[sem],
+            src_ref=src, dst_ref=dst, send_sem=out_send.at[sem // NCH], recv_sem=out_recv.at[sem],
             device_id=device(along(axis, step), lax.rem(core + flip, 2)), device_id_type=MESH,
         ).start()
 
@@ -362,6 +362,25 @@
     def of(g):
         return range(3 * g, 3 * g + 3)
 
+    def spread(stage, own, slots, targets):
+        first_slot = (0, 8, 12)[stage]
+        sums[first_slot + own] = volume_parts[stage]
+        for target in targets:
+            pltpu.make_async_remote_copy(
+                src_ref=sums.at[first_slot + own], dst_ref=sums.at[first_slot + own],
+                send_sem=sum_send.at[stage], recv_sem=sum_recv.at[stage],
+                device_id=target, device_id_type=MESH,
+            ).start()
+
+    def collect(stage, slots):
+        first_slot = (0, 8, 12)[stage]
+        for sem in (sum_recv, sum_send):
+            wait(sem.at[stage], sums.at[pl.ds(first_slot, slots - 1)])
+        out = sums[first_slot]
+        for s in range(1, slots):
+            out = out + sums[first_slot + s]
+        return out
+
     volume = jnp.zeros((8, BS), jnp.float32)
     for g in range(GROUPS):
         if g < 2:
@@ -377,43 +396,30 @@
             volume = lax.fori_loop(
                 0, SIDE, lambda n, acc, g=g: fill(g, n // 2, lax.rem(n, 2), acc), volume
             )
+            if g == GROUPS - 1:
+                volume_parts = [volume]
+                spread(
+                    0, x * 2 + core, 8,
+                    [
+                        device(along(0, s), lax.rem(core + k, 2))
+                        for s in range(SIDE) for k in range(2) if s or k
+                    ],
+                )
             for j in of(g):
                 hop1(j)
             for j in of(g - 1):
                 hop2(j)
 
-    def spread(stage, own, slots, targets):
-        first_slot = (0, 8, 12)[stage]
-        sums[first_slot + own] = volume_parts[stage]
-        for target in targets:
-            pltpu.make_async_remote_copy(
-                src_ref=sums.at[first_slot + own], dst_ref=sums.at[first_slot + own],
-                send_sem=sum_send.at[stage], recv_sem=sum_recv.at[stage],
-                device_id=target, device_id_type=MESH,
-            ).start()
-
-    def collect(stage, slots):
-        first_slot = (0, 8, 12)[stage]
-        for sem in (sum_recv, sum_send):
-            wait(sem.at[stage], sums.at[pl.ds(first_slot, slots - 1)])
-        out = sums[first_slot]
-        for s in range(1, slots):
-            out = out + sums[first_slot + s]
-        return out
-
-    volume_parts = [volume]
-    spread(
-        0, x * 2 + core, 8,
-        [device(along(0, s), lax.rem(core + k, 2)) for s in range(SIDE) for k in range(2) if s or k],
-    )
-    for j in range(NCH - 3, NCH):
-        hop2(j)
     volume_parts.append(collect(0, 8))
     spread(1, y, 4, [device(along(1, s), core) for s in range(1, SIDE)])
-    for j in range(NCH):
+    for j in of(GROUPS - 1):
+        hop2(j)
+    for j in range(NCH - 3):
         hop3(j)
     volume_parts.append(collect(1, 4))
     spread(2, z, 4, [device(along(2, s), core) for s in range(1, SIDE)])
+    for j in of(GROUPS - 1):
+        hop3(j)
     all_volume = jnp.sum(collect(2, 4))
     cells = float(ROWS * COLS * 128)
     constraint = all_volume / cells / VOLUME_TARGET - 1.0
@@ -421,12 +427,10 @@
 
     for j in range(NCH):
         wait(out_recv.at[2 * NCH + j], got3(j))
-    for j in range(NCH):
-        wait(out_send.at[j], got1(j))
-        wait(out_send.at[NCH + j], got2(j))
-        wait(out_send.at[2 * NCH + j], got3(j))
-        g, flip, (a, b, c), begin, rows = CHUNKS[j]
-        wait(local_sem.at[0], view(arrived, g, {c: HOME}, begin, rows))
+    wait(out_send.at[0], mid1.at[:, :, :, :, pl.ds(0, BS * 7 // 8)])
+    wait(out_send.at[1], mid2.at[:, OTHERS])
+    wait(out_send.at[2], arrived.at[:, OTHERS])
+    wait(local_sem.at[0], arrived.at[:, HOME])
     for copy in halo:
         copy.wait_send()
 
@@ -478,8 +482,8 @@
             *[pltpu.VMEM(exchange, jnp.bfloat16)] * 3,
             pltpu.VMEM((2, BS, BS), jnp.float32), pltpu.VMEM((2, BS, BS), jnp.float32),
             pltpu.VMEM((16, 8, BS), jnp.float32),
-            dma((KC,)), dma((3,)), dma((1,)), dma((8,)), dma((8,)), dma((3,)), dma((3,)),
-            dma((3 * NCH,)), dma((3 * NCH,)), dma((1,)),
+            dma((3,)), dma((3,)), dma((1,)), dma((8,)), dma((8,)), dma((3,)), dma((3,)),
+            dma((3,)), dma((3 * NCH,)), dma((1,)),
         ],
         compiler_params=pltpu.CompilerParams(
             collective_id=0, has_side_effects=True, vmem_limit_bytes=54 * 2**20

time: 119 us -> 119 us (level)
  no operation moved by 1% of the time
where the time goes in v3:
time: 119 us; the launch traced here: 118 us
  Pallas kernels  118 us (99%)
    pallas_call x1, Pallas kernels, per_device(): pl.pallas_call(fused_kernel, out_shape=(pltpu.VMEM(exchange, jnp.bfloat16...  113 us
    pallas_call x1, Pallas kernels, per_device(): pl.pallas_call(place_kernel, out_shape=(jax.ShapeDtypeStruct((KR * KC, BS...  4.39 us

profile of v3, /device:TPU:0, one launch (start us, length us, event | category | flops | bytes accessed | tf_op | source)
XLA Modules:
  0.0 118.4 jit_solution(1513474291013112244)
XLA Ops:
  0.6 113.2 %filter_exchange.1 = (bf16[4,4,4,4,128,128]{5,4,3,2,1,0:T(8,128)(2,1)S(1)}, s32[8,128]{1,0:T(8,128)S(1)}, f32[8,128]{1,0:T(8,128)S(1)}) custom-call(f32[64,16,4096]{2,1,0:T(8,128)} %bitcast.3, s32[256,128]{1,0:T(8,128)} %bitcast.4, bf16[256,320]{1,0:T(8,128)(2,1)} %constant.4.clone.w_row_in, bf16[512,256]{1,0:T(8,128)(2,1)} %constant.5.clone.w_col_in, ...), custom_call_target="tpu_custom_call" | custom-call | tf_op jit(solution)/shard_map/filter_exchange/pallas_call | solution.py:466
  113.8 4.4 %place_blocks.1 = (bf16[256,128,128]{2,1,0:T(8,128)(2,1)}, f32[1,1]{1,0:T(1,128)}) custom-call(s32[8,128]{1,0:T(8,128)S(1)} %get-tuple-element.7.slots, f32[8,128]{1,0:T(8,128)S(1)} %get-tuple-element.8.total, bf16[4,4,4,4,128,128]{5,4,3,2,1,0:T(8,128)(2,1)S(1)} %get-tuple-element.9.arrived), custom_call_target="tpu_custom_call" | custom-call | tf_op jit(solution)/shard_map/place_blocks/pallas_call | solution.py:496
